TPU v7x, 32 devices: a whole 2x2x4 slice. The times are simulated.
32 devices in a mesh: row: 4 (over x, core), col: 8 (over z, y).
Axes of the slice: x: 2, y: 2, z: 4, core: 2. Of those that a mesh axis runs over, the one named last changes fastest.
Arguments:
- vectors: float32 [32768, 768], P(('row', 'col')), may hold values from -6 to 6
- list_ids: int32 [32768], P(('row', 'col')), may hold values from 0 to 16383, as said below
- pq_codes: int32 [32768, 96], P(('row', 'col')), may hold values from 0 to 255
- fill_counts: int32 [32, 32], P(('row', 'col')), may hold values from 0 to 32, as said below
- centroids: float32 [16384, 768], P(('row', 'col')), may hold values from -6 to 6
- codebook: float32 [96, 8, 256], P('col'), may hold values from -6 to 6
Outputs:
- coded_err: float32 [32768], P(('row', 'col'))
- best_err: float32 [32768], P(('row', 'col'))
Inputs may be any that keep to these rules, and one draw needn't show every extreme that they name: `list_ids`: slot s of device p lies in block s // 32, which belongs to owner device s // 32 (devices numbered row-major over row and col); it names a list of that owner, from (s // 32) * 512 to (s // 32 + 1) * 512 - 1. fill_counts[p, d] is the number of live slots at the head of device p's block for owner d; some owner receives 32 live slots from every device.
All inputs are finite; a program needn't handle non-finite values.
Results may differ from a plain program's by a relative error of at most 0.0003.
Values sent between devices are 32-bit elements; how exact they have to be, the bound alone decides.
A program may use at most 256 MiB of HBM per device.

v0:
```python
import functools

import jax
import jax.numpy as jnp
from jax import lax
from jax.experimental import pallas as pl
from jax.experimental.pallas import tpu as pltpu
from jax.sharding import PartitionSpec as P

F32 = jnp.float32
BF16 = jnp.bfloat16
DEPTH = 64


def split3(x):
    hi = x.astype(BF16).astype(F32)
    rest = x - hi
    mid = rest.astype(BF16).astype(F32)
    return hi, mid, rest - mid


def build_table(cb_ref, w_ref):
    sub_count, sub_width, code_count = cb_ref.shape

    def step(m, carry):
        c = cb_ref[m]
        hi, mid, lo = split3(-2.0 * c)
        norm = jnp.sum(c * c, axis=0, keepdims=True)
        nh, nm, nl = split3(norm)
        line = lax.broadcasted_iota(jnp.int32, c.shape, 0)
        norms = jnp.where(line == 0, nh, jnp.where(line == 1, nm, jnp.where(line == 2, nl, 0.0)))
        pieces = [hi, hi, hi, mid, mid, lo, norms, jnp.zeros_like(c)]
        w_ref[m] = jnp.concatenate(pieces, axis=0).T.astype(BF16)
        return carry

    lax.fori_loop(0, sub_count, step, 0, unroll=4)


def pick(row, code, sub_width):
    lanes = code.shape[1]
    outs = []
    for start in range(0, lanes, 128):
        idx = jnp.broadcast_to(code[:, start:start + 128], (sub_width, 128))
        low = jnp.bitwise_and(idx, 127)
        got = None
        for part in range(row.shape[1] // 128):
            piece = jnp.take_along_axis(
                row[:, part * 128:(part + 1) * 128], low, axis=1, mode="promise_in_bounds"
            )
            got = piece if got is None else jnp.where(idx >= part * 128, piece, got)
        outs.append(got)
    return jnp.concatenate(outs, axis=1)


def score(rt_ref, codes_ref, cb_ref, w_ref):
    sub_count, sub_width, code_count = cb_ref.shape
    width = rt_ref.shape[1]
    ones = jnp.ones((sub_width, width), F32)
    zeros = jnp.zeros((sub_width, width), F32)

    def step(g, carry):
        coded, norm, best = carry
        codes = codes_ref[pl.ds(pl.multiple_of(g * 8, 8), 8), :]
        for i in range(8):
            m = g * 8 + i
            r = rt_ref[pl.ds(pl.multiple_of(m * sub_width, sub_width), sub_width), :]
            hi, mid, lo = split3(r)
            x = jnp.concatenate([hi, mid, lo, hi, mid, hi, ones, zeros], axis=0).astype(BF16)
            table = jnp.dot(w_ref[m], x, preferred_element_type=F32)
            best = best + jnp.min(table, axis=0, keepdims=True)
            norm = norm + r * r
            diff = r - pick(cb_ref[m], codes[i:i + 1, :], sub_width)
            coded = coded + diff * diff
        return coded, norm, best

    coded, norm, best = lax.fori_loop(
        0, sub_count // 8, step, (zeros, zeros, jnp.zeros((1, width), F32))
    )
    coded = jnp.sum(coded, axis=0, keepdims=True)
    best = best + jnp.sum(norm, axis=0, keepdims=True)
    return coded, best


def exchange_kernel(row_count, col_count, wanted_ref, cb_ref, v_ref, codes_ref, coded_ref, best_ref,
                    got_ref, book_ref, w_ref, rt_ref, first_send, second_send, book_recv, rows_send, rows_recv):
    row = lax.axis_index("row")
    col = lax.axis_index("col")
    sub_local = cb_ref.shape[0]
    width = rt_ref.shape[1]
    capacity = width // col_count
    groups = col_count // row_count

    def other_row(step):
        return lax.rem(row + step + row_count, row_count)

    def other_col(step):
        return lax.rem(col + step + col_count, col_count)

    def piece(j):
        return book_ref.at[pl.ds(j * sub_local, sub_local)]

    def block(ref, r, c):
        start = pl.multiple_of((r * col_count + c) * capacity, capacity)
        return ref.at[pl.ds(start, capacity)]

    def first_copy(step):
        return pltpu.make_async_remote_copy(
            src_ref=cb_ref, dst_ref=piece(col), send_sem=first_send.at[step], recv_sem=book_recv.at[col],
            device_id=(row, other_col(step)), device_id_type=pl.DeviceIdType.MESH)

    def second_copy(group, step):
        j = group * row_count + row
        return pltpu.make_async_remote_copy(
            src_ref=piece(j), dst_ref=piece(j), send_sem=second_send.at[group, step], recv_sem=book_recv.at[j],
            device_id=(other_row(step), col), device_id_type=pl.DeviceIdType.MESH)

    def arrived(j):
        return pltpu.make_async_remote_copy(
            src_ref=cb_ref, dst_ref=piece(j), send_sem=first_send.at[0], recv_sem=book_recv.at[j],
            device_id=(row, other_col(1)), device_id_type=pl.DeviceIdType.MESH)

    def rows_copy(row_step, col_step):
        r, c = other_row(row_step), other_col(col_step)
        slot = row_step * col_count + col_step
        return pltpu.make_async_remote_copy(
            src_ref=block(wanted_ref, r, c), dst_ref=block(got_ref, row, col),
            send_sem=rows_send.at[slot], recv_sem=rows_recv.at[slot],
            device_id=(r, c), device_id_type=pl.DeviceIdType.MESH)

    def rows_arrived(row_step, col_step):
        r, c = other_row(-row_step), other_col(-col_step)
        slot = row_step * col_count + col_step
        return pltpu.make_async_remote_copy(
            src_ref=block(wanted_ref, r, c), dst_ref=block(got_ref, r, c),
            send_sem=rows_send.at[slot], recv_sem=rows_recv.at[slot],
            device_id=(other_row(row_step), other_col(col_step)), device_id_type=pl.DeviceIdType.MESH)

    spreads = lax.rem(col, row_count) == row

    @pl.when(spreads)
    def _():
        for step in range(1, col_count):
            first_copy(step).start()

    book_ref[pl.ds(col * sub_local, sub_local)] = cb_ref[...]
    own = pl.multiple_of((row * col_count + col) * capacity, capacity)
    got_ref[pl.ds(own, capacity), :] = wanted_ref[pl.ds(own, capacity), :]
    for group in range(groups):
        @pl.when(group * row_count + row != col)
        def _(group=group):
            arrived(group * row_count + row).wait_recv()
            for step in range(1, row_count):
                second_copy(group, step).start()

    pairs = [(a, b) for a in range(row_count) for b in range(col_count) if a + b > 0]
    for a, b in pairs:
        rows_copy(a, b).start()

    for group in range(groups):
        for step in range(1, row_count):
            j = group * row_count + other_row(-step)

            @pl.when(j != col)
            def _(j=j):
                arrived(j).wait_recv()
    build_table(book_ref, w_ref)

    for a in range(row_count):
        for b in range(col_count):
            if a + b > 0:
                rows_arrived(a, b).wait_recv()
        base = pl.multiple_of(other_row(-a) * width, width)
        rt_ref[...] = (v_ref[pl.ds(base, width), :] - got_ref[pl.ds(base, width), :]).T
        coded, best = score(rt_ref, codes_ref.at[:, pl.ds(base, width)], book_ref, w_ref)
        coded_ref[:, pl.ds(base, width)] = coded
        best_ref[:, pl.ds(base, width)] = best

    @pl.when(spreads)
    def _():
        for step in range(1, col_count):
            first_copy(step).wait_send()

    for group in range(groups):
        @pl.when(group * row_count + row != col)
        def _(group=group):
            for step in range(1, row_count):
                second_copy(group, step).wait_send()
    for a, b in pairs:
        rows_copy(a, b).wait_send()


def local(vectors, list_ids, pq_codes, fill_counts, centroids, codebook):
    row_count = lax.axis_size("row")
    col_count = lax.axis_size("col")
    device_count = row_count * col_count
    slot_count, feature_width = vectors.shape
    capacity = slot_count // device_count
    sub_total = pq_codes.shape[1]
    sub_width, code_count = codebook.shape[1:]
    axes = ("row", "col")
    swap = functools.partial(lax.all_to_all, axis_name=axes, split_axis=0, concat_axis=0, tiled=True)

    got_ids = swap(list_ids.reshape(device_count, capacity)).reshape(slot_count)
    wanted = jnp.take(centroids, got_ids % centroids.shape[0], axis=0, mode="clip")
    width = slot_count // row_count
    vmem = pl.BlockSpec(memory_space=pltpu.VMEM)
    coded, best = pl.pallas_call(
        functools.partial(exchange_kernel, row_count, col_count),
        out_shape=[jax.ShapeDtypeStruct((1, slot_count), F32)] * 2,
        in_specs=[vmem] * 4,
        out_specs=[vmem] * 2,
        scratch_shapes=[
            pltpu.VMEM((slot_count, feature_width), F32),
            pltpu.VMEM((sub_total, sub_width, code_count), F32),
            pltpu.VMEM((sub_total, code_count, DEPTH), BF16),
            pltpu.VMEM((feature_width, width), F32),
            pltpu.SemaphoreType.DMA((col_count,)),
            pltpu.SemaphoreType.DMA((col_count // row_count, row_count)),
            pltpu.SemaphoreType.DMA((col_count,)),
            pltpu.SemaphoreType.DMA((device_count,)),
            pltpu.SemaphoreType.DMA((device_count,)),
        ],
        compiler_params=pltpu.CompilerParams(has_side_effects=True, vmem_limit_bytes=48 * 2**20),
        name="exchange_score",
    )(wanted, codebook, vectors, pq_codes.T)

    slot_pos = jnp.arange(capacity, dtype=jnp.int32)
    live = (slot_pos[None, :] < fill_counts[0][:, None]).reshape(slot_count)
    coded_err = jnp.where(live, coded.reshape(slot_count), 0.0)
    best_err = jnp.where(live, best.reshape(slot_count), 0.0)
    return (coded_err, best_err)


def solution(mesh):
    in_specs = (
        P(("row", "col"), None),
        P(("row", "col")),
        P(("row", "col"), None),
        P(("row", "col"), None),
        P(("row", "col"), None),
        P("col", None, None),
    )
    out_specs = (P(("row", "col")), P(("row", "col")))
    return jax.shard_map(local, mesh=mesh, in_specs=in_specs, out_specs=out_specs, check_vma=False)
```

profile of v0, /device:TPU:13, one launch (start us, length us, event | category | flops | bytes accessed | tf_op | source)
XLA Modules:
  0.0 111.8 jit_solution(13299204103799797886)
XLA Ops:
  0.6 0.0 copy-start
  0.6 1.5 %all_to_all.6 = s32[32,1,32]{2,1,0:T(1,128)} reshape(s32[1024]{0:T(1024)} %param.7) | data formatting | bytes 8192 | tf_op jit(solution)/shard_map/all_to_all | solution.py:203
  2.1 6.3 %all-to-all-start = ((s32[32,1,32]{2,1,0:T(1,128)}), s32[32,1,32]{2,1,0:T(1,128)S(1)}, u32[]{:S(2)}, u32[]{:S(2)}) async-start(s32[32,1,32]{2,1,0:T(1,128)} %all_to_all.6), calls=%async_computation | async-start | bytes 32768 | tf_op jit(solution)/shard_map/all_to_all | solution.py:203
  8.4 0.7 iota_compare_fusion
  9.1 0.1 lt.29
  9.2 4.0 %all-to-all-done = s32[32,1,32]{2,1,0:T(1,128)S(1)} async-done(((s32[32,1,32]{2,1,0:T(1,128)}), s32[32,1,32]{2,1,0:T(1,128)S(1)}, u32[]{:S(2)}, u32[]{:S(2)}) %all-to-all-start) | async-done | bytes 4128 | tf_op jit(solution)/shard_map/all_to_all | solution.py:203
  13.2 0.5 broadcast.51
  13.7 0.7 reduce.3
  14.4 0.1 reshape.75
  14.5 0.0 copy-done
  14.5 0.0 copy-start.2
  14.5 0.0 copy-start.3
  14.5 5.3 %gather_fusion = f32[1024,768]{1,0:T(8,128)} fusion(f32[512,768]{1,0:T(8,128)S(1)} %copy-done, s32[1024]{0:T(1024)S(1)} %broadcast_clamp_fusion), kind=kCustom, calls=%fused_computation | custom fusion | bytes 6295552 | tf_op jit(solution)/shard_map/jit(_take)/gather | solution.py:204
  19.8 0.0 copy-done.2
  19.8 0.0 copy-done.3
  19.8 0.0 copy-start.1
  19.8 1.9 %copy-done.1 = f32[1024,768]{1,0:T(8,128)S(1)} copy-done((f32[1024,768]{1,0:T(8,128)S(1)}, f32[1024,768]{1,0:T(8,128)}, u32[]{:S(2)}) %copy-start.1) | copy-done | bytes 3145752
  21.7 89.5 %exchange_score.1 = (f32[1,1024]{1,0:T(1,128)S(1)}, f32[1,1024]{1,0:T(1,128)S(1)}) custom-call(f32[1024,768]{1,0:T(8,128)S(1)} %copy-done.1, f32[12,8,256]{2,1,0:T(8,128)S(1)} %copy-done.3, f32[1024,768]{1,0:T(8,128)} %v_ref.1, s32[96,1024]{1,0:T(8,128)S(1)} %bitcast.5), custom_call_target="tpu_custom_call" | custom-call | tf_op jit(solution)/shard_map/exchange_score/pallas_call | solution.py:207
  111.2 0.6 broadcast_select_fusion
  (2 shorter events, 0.0 us)
Async XLA Ops:
  0.6 13.9 %copy-start = (f32[512,768]{1,0:T(8,128)S(1)}, f32[512,768]{1,0:T(8,128)}, u32[]{:S(2)}) copy-start(f32[512,768]{1,0:T(8,128)} %param.10) | copy-start | bytes 4718596
  2.1 11.1 %all-to-all-start = ((s32[32,1,32]{2,1,0:T(1,128)}), s32[32,1,32]{2,1,0:T(1,128)S(1)}, u32[]{:S(2)}, u32[]{:S(2)}) async-start(s32[32,1,32]{2,1,0:T(1,128)} %all_to_all.6), calls=%async_computation | async-start | bytes 32768 | tf_op jit(solution)/shard_map/all_to_all | solution.py:203
  14.5 5.3 %copy-start.2 = (s32[1024,96]{0,1:T(8,128)S(1)}, s32[1024,96]{0,1:T(8,128)}, u32[]{:S(2)}) copy-start(s32[1024,96]{0,1:T(8,128)} %param.8) | copy-start | bytes 1179652
  14.5 5.3 %copy-start.3 = (f32[12,8,256]{2,1,0:T(8,128)S(1)}, f32[12,8,256]{2,1,0:T(8,128)}, u32[]{:S(2)}) copy-start(f32[12,8,256]{2,1,0:T(8,128)} %cb_ref.1) | copy-start | bytes 294916
  19.8 1.9 %copy-start.1 = (f32[1024,768]{1,0:T(8,128)S(1)}, f32[1024,768]{1,0:T(8,128)}, u32[]{:S(2)}) copy-start(f32[1024,768]{1,0:T(8,128)} %gather_fusion) | copy-start | bytes 9437188
where the time goes:
time: 112 us
  Pallas kernels  89.5 us (80%)
  local copies, waits for them, and re-layouts  9.36 us (8%)
  starting transfers between devices  6.27 us (6%)
  waiting for transfers between devices  3.96 us (4%)
  other arithmetic  2.04 us (2%)
    pallas_call x1, Pallas kernels, local(): pl.pallas_call(functools.partial(exchange_kernel, row_count, col_count),...  89.5 us
    all_to_all x1, starting transfers between devices, local(): got_ids = swap(list_ids.reshape(device_count, capacity)).reshape(slot_count)  6.27 us
    gather x1, local copies, waits for them, and re-layouts, local(): jnp.take(centroids, got_ids % centroids.shape[0], axis=0, mode='clip')  5.29 us
    all_to_all x1, waiting for transfers between devices, local(): got_ids = swap(list_ids.reshape(device_count, capacity)).reshape(slot_count)  3.96 us
  transfers between devices with their start and end apart: 1, of which 1 were waited for; matrix products, arithmetic and copies ran while one was open for 1% of the time, Pallas kernels for 0%

commit v1 on v0

v1 whole, which is shorter than its diff:
```python
import functools

import jax
import jax.numpy as jnp
from jax import lax
from jax.experimental import pallas as pl
from jax.experimental.pallas import tpu as pltpu
from jax.sharding import PartitionSpec as P

F32 = jnp.float32
BF16 = jnp.bfloat16
DEPTH = 64
LANES = 128
PAIRS = 8


def xor(i, s, count):
    out = 0
    bit = 1
    while bit < count:
        out = out + bit * lax.rem(lax.div(i, bit) + lax.div(s, bit), 2)
        bit *= 2
    return out


def split3(x):
    hi = x.astype(BF16).astype(F32)
    rest = x - hi
    mid = rest.astype(BF16).astype(F32)
    return hi, mid, rest - mid


def code_rows(c):
    hi, mid, lo = split3(-2.0 * c)
    norm = jnp.sum(c * c, axis=0, keepdims=True)
    nh, nm, nl = split3(norm)
    line = lax.broadcasted_iota(jnp.int32, c.shape, 0)
    norms = jnp.where(line == 0, nh, jnp.where(line == 1, nm, jnp.where(line == 2, nl, 0.0)))
    return [hi, hi, hi, mid, mid, lo, norms, jnp.zeros_like(c)]


def build_table(cb_ref, w_ref):
    def step(i, carry):
        pieces = code_rows(cb_ref[2 * i]) + code_rows(cb_ref[2 * i + 1])
        w_ref[i] = jnp.concatenate(pieces, axis=0).T.astype(BF16)
        return carry

    lax.fori_loop(0, w_ref.shape[0], step, 0, unroll=2)


def pick(row, idx):
    low = jnp.bitwise_and(idx, LANES - 1)
    got = None
    for part in range(row.shape[1] // LANES):
        piece = jnp.take_along_axis(
            row[:, part * LANES:(part + 1) * LANES], low, axis=1, mode="promise_in_bounds"
        )
        got = piece if got is None else jnp.where(idx >= part * LANES, piece, got)
    return got


def score(rt_ref, codes_ref, base, cb_ref, w_ref):
    sub_count, sub_width, _ = cb_ref.shape
    ones = jnp.ones((sub_width, LANES), F32)
    zeros = jnp.zeros((sub_width, LANES), F32)
    blank = jnp.zeros((DEPTH, LANES), BF16)

    def side(m, code):
        r = rt_ref[pl.ds(pl.multiple_of(m * sub_width, sub_width), sub_width), :]
        hi, mid, lo = split3(r)
        x = jnp.concatenate([hi, mid, lo, hi, mid, hi, ones, zeros], axis=0).astype(BF16)
        diff = r - pick(cb_ref[m], jnp.broadcast_to(code, (sub_width, LANES)))
        return x, r * r, diff * diff

    def step(g, carry):
        coded, norm, best = carry
        codes = codes_ref[pl.ds(pl.multiple_of(g * 2 * PAIRS, 8), 2 * PAIRS), pl.ds(base, LANES)]
        for i in range(PAIRS):
            pair = g * PAIRS + i
            xa, na, da = side(2 * pair, codes[2 * i:2 * i + 1, :])
            xb, nb, db = side(2 * pair + 1, codes[2 * i + 1:2 * i + 2, :])
            x = jnp.concatenate(
                [jnp.concatenate([xa, blank], axis=1), jnp.concatenate([blank, xb], axis=1)], axis=0)
            table = jnp.dot(w_ref[pair], x, preferred_element_type=F32)
            best = best + jnp.min(table, axis=0, keepdims=True)
            norm = norm + (na + nb)
            coded = coded + (da + db)
        return coded, norm, best

    coded, norm, best = lax.fori_loop(
        0, sub_count // (2 * PAIRS), step, (zeros, zeros, jnp.zeros((1, 2 * LANES), F32))
    )
    coded = jnp.sum(coded, axis=0, keepdims=True)
    best = best[:, :LANES] + best[:, LANES:] + jnp.sum(norm, axis=0, keepdims=True)
    return coded, best


def exchange_kernel(row_count, col_count, cb_hbm, v_hbm, codes_hbm, cent_hbm, ids_ref, fill_ref,
                    coded_ref, best_ref,
                    wanted_ref, got_ref, v_ref, cent_ref, codes_ref, book_ref, w_ref, rt_ref, ids_sm,
                    local_sem, ids_send, ids_recv, first_send, second_send, book_recv, rows_send, rows_recv):
    row = lax.axis_index("row")
    col = lax.axis_index("col")
    me = row * col_count + col
    count = row_count * col_count
    sub_local = cb_hbm.shape[0]
    slot_count = v_ref.shape[0]
    capacity = slot_count // count
    lists = cent_ref.shape[0]
    groups = col_count // row_count
    per = LANES // capacity
    spans = col_count // per

    def place(slot):
        return xor(row, lax.div(slot, col_count), row_count), xor(col, lax.rem(slot, col_count), col_count)

    def piece(j):
        return book_ref.at[pl.ds(j * sub_local, sub_local)]

    def block(ref, owner):
        return ref.at[pl.ds(pl.multiple_of(owner * capacity, capacity), capacity)]

    cent_copy = pltpu.make_async_copy(cent_hbm, cent_ref, local_sem.at[0])
    book_copy = pltpu.make_async_copy(cb_hbm, piece(col), local_sem.at[1])
    v_copy = pltpu.make_async_copy(v_hbm, v_ref, local_sem.at[2])
    codes_copy = pltpu.make_async_copy(codes_hbm, codes_ref, local_sem.at[3])
    book_copy.start()
    cent_copy.start()
    v_copy.start()
    codes_copy.start()

    barrier = pltpu.get_barrier_semaphore()

    def greet(slot, carry):
        r, c = place(slot)
        pl.semaphore_signal(barrier, inc=1, device_id=(r, c), device_id_type=pl.DeviceIdType.MESH)
        return carry

    lax.fori_loop(1, count, greet, 0)
    pl.semaphore_wait(barrier, count - 1)

    def ids_copy(slot):
        r, c = place(slot)
        line = lax.div((r * col_count + c) * capacity, LANES)
        return pltpu.make_async_remote_copy(
            src_ref=ids_ref.at[pl.ds(line, 1)], dst_ref=ids_sm.at[pl.ds(me, 1)],
            send_sem=ids_send.at[slot], recv_sem=ids_recv.at[slot],
            device_id=(r, c), device_id_type=pl.DeviceIdType.MESH)

    def ids_arrived(slot):
        r, c = place(slot)
        return pltpu.make_async_remote_copy(
            src_ref=ids_ref.at[pl.ds(0, 1)], dst_ref=ids_sm.at[pl.ds(r * col_count + c, 1)],
            send_sem=ids_send.at[slot], recv_sem=ids_recv.at[slot],
            device_id=(r, c), device_id_type=pl.DeviceIdType.MESH)

    def send_ids(i, carry):
        ids_copy(count - 1 - i).start()
        return carry

    lax.fori_loop(0, count - 1, send_ids, 0)
    own_ids = pltpu.make_async_copy(
        ids_ref.at[pl.ds(lax.div(me * capacity, LANES), 1)], ids_sm.at[pl.ds(me, 1)], local_sem.at[4])
    own_ids.start()

    def first_copy(step):
        return pltpu.make_async_remote_copy(
            src_ref=piece(col), dst_ref=piece(col), send_sem=first_send.at[step], recv_sem=book_recv.at[col],
            device_id=(row, lax.rem(col + step, col_count)), device_id_type=pl.DeviceIdType.MESH)

    def second_copy(group, step):
        j = group * row_count + row
        return pltpu.make_async_remote_copy(
            src_ref=piece(j), dst_ref=piece(j), send_sem=second_send.at[group, step], recv_sem=book_recv.at[j],
            device_id=(lax.rem(row + step, row_count), col), device_id_type=pl.DeviceIdType.MESH)

    def arrived(j):
        return pltpu.make_async_remote_copy(
            src_ref=piece(col), dst_ref=piece(j), send_sem=first_send.at[0], recv_sem=book_recv.at[j],
            device_id=(row, lax.rem(col + 1, col_count)), device_id_type=pl.DeviceIdType.MESH)

    spreads = lax.rem(col, row_count) == row
    book_copy.wait()

    @pl.when(spreads)
    def _():
        for step in range(1, col_count):
            first_copy(step).start()

    offset = lax.rem(me * capacity, LANES)

    def gather(owner, out_ref):
        start = pl.multiple_of(owner * capacity, capacity)

        def some(q, carry):
            for k in range(8):
                j = q * 8 + k
                at = lax.rem(ids_sm[owner, offset + j], lists)
                out_ref[pl.ds(start + j, 1), :] = cent_ref[pl.ds(at, 1), :]
            return carry

        lax.fori_loop(0, capacity // 8, some, 0)

    def rows_copy(slot):
        r, c = place(slot)
        return pltpu.make_async_remote_copy(
            src_ref=block(wanted_ref, r * col_count + c), dst_ref=block(got_ref, me),
            send_sem=rows_send.at[slot], recv_sem=rows_recv.at[slot],
            device_id=(r, c), device_id_type=pl.DeviceIdType.MESH)

    def rows_arrived(slot):
        r, c = place(slot)
        return pltpu.make_async_remote_copy(
            src_ref=block(wanted_ref, me), dst_ref=block(got_ref, r * col_count + c),
            send_sem=rows_send.at[slot], recv_sem=rows_recv.at[slot],
            device_id=(r, c), device_id_type=pl.DeviceIdType.MESH)

    def serve(first, last):
        def one(slot, carry):
            r, c = place(slot)
            ids_arrived(slot).wait_recv()
            gather(r * col_count + c, wanted_ref)

            @pl.when(slot > first)
            def _():
                rows_copy(slot - 1).start()

            return carry

        lax.fori_loop(first, last, one, 0)

    cent_copy.wait()
    half = (row_count // 2) * col_count
    serve(1, half)
    own_ids.wait()
    gather(me, got_ref)
    rows_copy(half - 1).start()

    for group in range(groups):
        @pl.when(group * row_count + row != col)
        def _(group=group):
            arrived(group * row_count + row).wait_recv()
        for step in range(1, row_count):
            @pl.when(group * row_count + row != col)
            def _(group=group, step=step):
                second_copy(group, step).start()

    serve(half, count)
    v_copy.wait()
    codes_copy.wait()
    rows_copy(count - 1).start()

    for group in range(groups):
        for step in range(1, row_count):
            j = group * row_count + lax.rem(row - step + row_count, row_count)

            @pl.when(j != col)
            def _(j=j):
                arrived(j).wait_recv()
    build_table(book_ref, w_ref)

    lane = lax.broadcasted_iota(jnp.int32, (1, LANES), 1)

    def group_step(g, carry):
        a = lax.div(g, 2 * spans) * 2 + lax.rem(g, 2)
        h = lax.rem(lax.div(g, 2), spans)

        def settle(j, inner):
            slot = a * col_count + h * per + j

            @pl.when(slot > 0)
            def _():
                rows_arrived(slot).wait_recv()

            return inner

        lax.fori_loop(0, per, settle, 0)
        first = xor(row, a, row_count) * col_count + xor(lax.div(col, per), h, spans) * per
        base = pl.multiple_of(first * capacity, LANES)
        rt_ref[...] = (v_ref[pl.ds(base, LANES), :] - got_ref[pl.ds(base, LANES), :]).T
        coded, best = score(rt_ref, codes_ref, base, book_ref, w_ref)
        bound = jnp.zeros((1, LANES), jnp.int32)
        for j in range(per):
            bound = jnp.where(lane >= j * capacity, fill_ref[0, first + j] + j * capacity, bound)
        live = lane < bound
        coded_ref[:, pl.ds(base, LANES)] = jnp.where(live, coded, 0.0)
        best_ref[:, pl.ds(base, LANES)] = jnp.where(live, best, 0.0)
        return carry

    lax.fori_loop(0, row_count * spans, group_step, 0)

    @pl.when(spreads)
    def _():
        for step in range(1, col_count):
            first_copy(step).wait_send()

    for group in range(groups):
        @pl.when(group * row_count + row != col)
        def _(group=group):
            for step in range(1, row_count):
                second_copy(group, step).wait_send()

    def drain(slot, carry):
        ids_copy(slot).wait_send()
        rows_copy(slot).wait_send()
        return carry

    lax.fori_loop(1, count, drain, 0)


def local(vectors, list_ids, pq_codes, fill_counts, centroids, codebook):
    row_count = lax.axis_size("row")
    col_count = lax.axis_size("col")
    count = row_count * col_count
    slot_count, feature_width = vectors.shape
    sub_total = pq_codes.shape[1]
    sub_width, code_count = codebook.shape[1:]
    vmem = pl.BlockSpec(memory_space=pltpu.VMEM)
    smem = pl.BlockSpec(memory_space=pltpu.SMEM)
    hbm = pl.BlockSpec(memory_space=pl.ANY)
    coded, best = pl.pallas_call(
        functools.partial(exchange_kernel, row_count, col_count),
        out_shape=[jax.ShapeDtypeStruct((1, slot_count), F32)] * 2,
        in_specs=[hbm] * 4 + [vmem, smem],
        out_specs=[vmem] * 2,
        scratch_shapes=[
            pltpu.VMEM((slot_count, feature_width), F32),
            pltpu.VMEM((slot_count, feature_width), F32),
            pltpu.VMEM((slot_count, feature_width), F32),
            pltpu.VMEM(centroids.shape, F32),
            pltpu.VMEM((sub_total, slot_count), jnp.int32),
            pltpu.VMEM((sub_total, sub_width, code_count), F32),
            pltpu.VMEM((sub_total // 2, code_count, 2 * DEPTH), BF16),
            pltpu.VMEM((feature_width, LANES), F32),
            pltpu.SMEM((count, LANES), jnp.int32),
            pltpu.SemaphoreType.DMA((5,)),
            pltpu.SemaphoreType.DMA((count,)),
            pltpu.SemaphoreType.DMA((count,)),
            pltpu.SemaphoreType.DMA((col_count,)),
            pltpu.SemaphoreType.DMA((col_count // row_count, row_count)),
            pltpu.SemaphoreType.DMA((col_count,)),
            pltpu.SemaphoreType.DMA((count,)),
            pltpu.SemaphoreType.DMA((count,)),
        ],
        compiler_params=pltpu.CompilerParams(
            collective_id=0, has_side_effects=True, vmem_limit_bytes=56 * 2**20),
        name="exchange_score",
    )(codebook, vectors, pq_codes.T, centroids, list_ids.reshape(slot_count // LANES, LANES), fill_counts)
    return coded.reshape(slot_count), best.reshape(slot_count)


def solution(mesh):
    in_specs = (
        P(("row", "col"), None),
        P(("row", "col")),
        P(("row", "col"), None),
        P(("row", "col"), None),
        P(("row", "col"), None),
        P("col", None, None),
    )
    out_specs = (P(("row", "col")), P(("row", "col")))
    return jax.shard_map(local, mesh=mesh, in_specs=in_specs, out_specs=out_specs, check_vma=False)
```

time: 112 us -> 91.9 us (0.82)
  the two profiles are of different devices: /device:TPU:13 before, /device:TPU:19 now
where the time goes in v1:
time: 91.9 us; the launch traced here: 91.6 us
  Pallas kernels  88.5 us (96%)
  local copies, waits for them, and re-layouts  2.53 us (3%)
    pallas_call x1, Pallas kernels, local(): pl.pallas_call(functools.partial(exchange_kernel, row_count, col_count),...  88.5 us
    unnamed x2, local copies, waits for them, and re-layouts  2.53 us

profile of v1, /device:TPU:19, one launch (start us, length us, event | category | flops | bytes accessed | tf_op | source)
XLA Modules:
  0.0 91.6 jit_solution(6973006466133648085)
XLA Ops:
  0.6 88.5 %exchange_score.1 = (f32[1,1024]{1,0:T(1,128)}, f32[1,1024]{1,0:T(1,128)}) custom-call(f32[12,8,256]{2,1,0:T(8,128)} %cb_hbm.1, f32[1024,768]{1,0:T(8,128)} %v_hbm.1, s32[96,1024]{1,0:T(8,128)} %bitcast.4, f32[512,768]{1,0:T(8,128)} %cent_hbm.1, s32[8,128]{1,0:T(8,128)} %bitcast.5, s32[1,32]{1,0:T(1,128)} %fill_ref.1), custom_call_target="tpu_custom_call" | custom-call | tf_op jit(solution)/shard_map/exchange_score/pallas_call | solution.py:321
  89.1 1.3 %copy.10 = f32[1024]{0:T(1024)} copy(f32[1024]{0:T(1024)} %bitcast.7) | data formatting | bytes 8192
  90.4 1.3 %copy.11 = f32[1024]{0:T(1024)} copy(f32[1024]{0:T(1024)} %bitcast.6) | data formatting | bytes 8192

commit v2 on v1

--- a/solution.py
+++ b/solution.py
@@ -59,8 +59,8 @@
     return got
 
 
-def score(rt_ref, codes_ref, base, cb_ref, w_ref):
-    sub_count, sub_width, _ = cb_ref.shape
+def score_step(g, carry, rt_ref, codes_ref, base, cb_ref, w_ref):
+    sub_width = cb_ref.shape[1]
     ones = jnp.ones((sub_width, LANES), F32)
     zeros = jnp.zeros((sub_width, LANES), F32)
     blank = jnp.zeros((DEPTH, LANES), BF16)
@@ -72,33 +72,37 @@
         diff = r - pick(cb_ref[m], jnp.broadcast_to(code, (sub_width, LANES)))
         return x, r * r, diff * diff
 
-    def step(g, carry):
-        coded, norm, best = carry
-        codes = codes_ref[pl.ds(pl.multiple_of(g * 2 * PAIRS, 8), 2 * PAIRS), pl.ds(base, LANES)]
-        for i in range(PAIRS):
-            pair = g * PAIRS + i
-            xa, na, da = side(2 * pair, codes[2 * i:2 * i + 1, :])
-            xb, nb, db = side(2 * pair + 1, codes[2 * i + 1:2 * i + 2, :])
-            x = jnp.concatenate(
-                [jnp.concatenate([xa, blank], axis=1), jnp.concatenate([blank, xb], axis=1)], axis=0)
-            table = jnp.dot(w_ref[pair], x, preferred_element_type=F32)
-            best = best + jnp.min(table, axis=0, keepdims=True)
-            norm = norm + (na + nb)
-            coded = coded + (da + db)
-        return coded, norm, best
-
-    coded, norm, best = lax.fori_loop(
-        0, sub_count // (2 * PAIRS), step, (zeros, zeros, jnp.zeros((1, 2 * LANES), F32))
-    )
+    coded, norm, best = carry
+    codes = codes_ref[pl.ds(pl.multiple_of(g * 2 * PAIRS, 8), 2 * PAIRS), pl.ds(base, LANES)]
+    for i in range(PAIRS):
+        pair = g * PAIRS + i
+        xa, na, da = side(2 * pair, codes[2 * i:2 * i + 1, :])
+        xb, nb, db = side(2 * pair + 1, codes[2 * i + 1:2 * i + 2, :])
+        x = jnp.concatenate(
+            [jnp.concatenate([xa, blank], axis=1), jnp.concatenate([blank, xb], axis=1)], axis=0)
+        table = jnp.dot(w_ref[pair], x, preferred_element_type=F32)
+        best = best + jnp.min(table, axis=0, keepdims=True)
+        norm = norm + (na + nb)
+        coded = coded + (da + db)
+    return coded, norm, best
+
+
+def score_start(sub_width):
+    zeros = jnp.zeros((sub_width, LANES), F32)
+    return zeros, zeros, jnp.zeros((1, 2 * LANES), F32)
+
+
+def score_end(carry):
+    coded, norm, best = carry
     coded = jnp.sum(coded, axis=0, keepdims=True)
-    best = best[:, :LANES] + best[:, LANES:] + jnp.sum(norm, axis=0, keepdims=True)
-    return coded, best
+    return coded, best[:, :LANES] + best[:, LANES:] + jnp.sum(norm, axis=0, keepdims=True)
 
 
 def exchange_kernel(row_count, col_count, cb_hbm, v_hbm, codes_hbm, cent_hbm, ids_ref, fill_ref,
-                    coded_ref, best_ref,
+                    coded_ref, best_ref, live_ref,
                     wanted_ref, got_ref, v_ref, cent_ref, codes_ref, book_ref, w_ref, rt_ref, ids_sm,
-                    local_sem, ids_send, ids_recv, first_send, second_send, book_recv, rows_send, rows_recv):
+                    local_sem, ids_send, ids_recv, first_send, mirror_send, second_send, book_recv,
+                    rows_send, rows_recv, last_send, last_recv):
     row = lax.axis_index("row")
     col = lax.axis_index("col")
     me = row * col_count + col
@@ -110,6 +114,10 @@
     groups = col_count // row_count
     per = LANES // capacity
     spans = col_count // per
+    top = col_count // 2
+    mirror = xor(col, top, col_count)
+    steps = v_ref.shape[1] // LANES
+    last = count - per
 
     def place(slot):
         return xor(row, lax.div(slot, col_count), row_count), xor(col, lax.rem(slot, col_count), col_count)
@@ -163,10 +171,10 @@
         ids_ref.at[pl.ds(lax.div(me * capacity, LANES), 1)], ids_sm.at[pl.ds(me, 1)], local_sem.at[4])
     own_ids.start()
 
-    def first_copy(step):
-        return pltpu.make_async_remote_copy(
-            src_ref=piece(col), dst_ref=piece(col), send_sem=first_send.at[step], recv_sem=book_recv.at[col],
-            device_id=(row, lax.rem(col + step, col_count)), device_id_type=pl.DeviceIdType.MESH)
+    def book_copy_to(source, target, sem):
+        return pltpu.make_async_remote_copy(
+            src_ref=piece(source), dst_ref=piece(source), send_sem=sem, recv_sem=book_recv.at[source],
+            device_id=(row, target), device_id_type=pl.DeviceIdType.MESH)
 
     def second_copy(group, step):
         j = group * row_count + row
@@ -175,17 +183,19 @@
             device_id=(lax.rem(row + step, row_count), col), device_id_type=pl.DeviceIdType.MESH)
 
     def arrived(j):
-        return pltpu.make_async_remote_copy(
-            src_ref=piece(col), dst_ref=piece(j), send_sem=first_send.at[0], recv_sem=book_recv.at[j],
-            device_id=(row, lax.rem(col + 1, col_count)), device_id_type=pl.DeviceIdType.MESH)
+        return book_copy_to(j, mirror, first_send.at[0])
+
+    def spread(source, sems):
+        return [book_copy_to(source, xor(col, b, col_count), sems.at[b]) for b in range(1, top)]
 
     spreads = lax.rem(col, row_count) == row
     book_copy.wait()
 
     @pl.when(spreads)
     def _():
-        for step in range(1, col_count):
-            first_copy(step).start()
+        book_copy_to(col, mirror, first_send.at[0]).start()
+        for copy in spread(col, first_send):
+            copy.start()
 
     offset = lax.rem(me * capacity, LANES)
 
@@ -215,7 +225,23 @@
             send_sem=rows_send.at[slot], recv_sem=rows_recv.at[slot],
             device_id=(r, c), device_id_type=pl.DeviceIdType.MESH)
 
-    def serve(first, last):
+    def last_copy(j, f):
+        r, c = place(last + j)
+        part = pl.ds(pl.multiple_of(f * LANES, LANES), LANES)
+        return pltpu.make_async_remote_copy(
+            src_ref=block(wanted_ref, r * col_count + c).at[:, part], dst_ref=block(got_ref, me).at[:, part],
+            send_sem=last_send.at[f, j], recv_sem=last_recv.at[f, j],
+            device_id=(r, c), device_id_type=pl.DeviceIdType.MESH)
+
+    def last_arrived(j, f):
+        r, c = place(last + j)
+        part = pl.ds(pl.multiple_of(f * LANES, LANES), LANES)
+        return pltpu.make_async_remote_copy(
+            src_ref=block(wanted_ref, me).at[:, part], dst_ref=block(got_ref, r * col_count + c).at[:, part],
+            send_sem=last_send.at[f, j], recv_sem=last_recv.at[f, j],
+            device_id=(r, c), device_id_type=pl.DeviceIdType.MESH)
+
+    def serve(first, end):
         def one(slot, carry):
             r, c = place(slot)
             ids_arrived(slot).wait_recv()
@@ -223,11 +249,13 @@
 
             @pl.when(slot > first)
             def _():
-                rows_copy(slot - 1).start()
+                @pl.when(slot <= last)
+                def _():
+                    rows_copy(slot - 1).start()
 
             return carry
 
-        lax.fori_loop(first, last, one, 0)
+        lax.fori_loop(first, end, one, 0)
 
     cent_copy.wait()
     half = (row_count // 2) * col_count
@@ -236,19 +264,33 @@
     gather(me, got_ref)
     rows_copy(half - 1).start()
 
+    @pl.when(spreads)
+    def _():
+        arrived(mirror).wait_recv()
+        for copy in spread(mirror, mirror_send):
+            copy.start()
+
     for group in range(groups):
-        @pl.when(group * row_count + row != col)
+        j = group * row_count + row
+
+        @pl.when((j - col) * (j - mirror) != 0)
+        def _(j=j):
+            arrived(j).wait_recv()
+
+        @pl.when(j != col)
         def _(group=group):
-            arrived(group * row_count + row).wait_recv()
-        for step in range(1, row_count):
-            @pl.when(group * row_count + row != col)
-            def _(group=group, step=step):
+            for step in range(1, row_count):
                 second_copy(group, step).start()
 
     serve(half, count)
     v_copy.wait()
     codes_copy.wait()
-    rows_copy(count - 1).start()
+
+    def send_last(i, carry):
+        last_copy(lax.rem(i, per), lax.div(i, per)).start()
+        return carry
+
+    lax.fori_loop(0, per * steps, send_last, 0)
 
     for group in range(groups):
         for step in range(1, row_count):
@@ -260,39 +302,60 @@
     build_table(book_ref, w_ref)
 
     lane = lax.broadcasted_iota(jnp.int32, (1, LANES), 1)
-
-    def group_step(g, carry):
+    sub_width = book_ref.shape[1]
+
+    def group_at(g):
         a = lax.div(g, 2 * spans) * 2 + lax.rem(g, 2)
         h = lax.rem(lax.div(g, 2), spans)
-
-        def settle(j, inner):
-            slot = a * col_count + h * per + j
-
-            @pl.when(slot > 0)
-            def _():
-                rows_arrived(slot).wait_recv()
-
-            return inner
-
-        lax.fori_loop(0, per, settle, 0)
         first = xor(row, a, row_count) * col_count + xor(lax.div(col, per), h, spans) * per
-        base = pl.multiple_of(first * capacity, LANES)
-        rt_ref[...] = (v_ref[pl.ds(base, LANES), :] - got_ref[pl.ds(base, LANES), :]).T
-        coded, best = score(rt_ref, codes_ref, base, book_ref, w_ref)
+        return a * col_count + h * per, first, pl.multiple_of(first * capacity, LANES)
+
+    def finish(carry, first, base):
+        coded, best = score_end(carry)
         bound = jnp.zeros((1, LANES), jnp.int32)
         for j in range(per):
             bound = jnp.where(lane >= j * capacity, fill_ref[0, first + j] + j * capacity, bound)
-        live = lane < bound
-        coded_ref[:, pl.ds(base, LANES)] = jnp.where(live, coded, 0.0)
-        best_ref[:, pl.ds(base, LANES)] = jnp.where(live, best, 0.0)
-        return carry
-
-    lax.fori_loop(0, row_count * spans, group_step, 0)
+        coded_ref[:, pl.ds(base, LANES)] = coded
+        best_ref[:, pl.ds(base, LANES)] = best
+        live_ref[:, pl.ds(base, LANES)] = jnp.where(lane < bound, 1, 0)
+
+    def group_step(g, carry):
+        slot, first, base = group_at(g)
+
+        def settle(j, inner):
+            @pl.when(slot + j > 0)
+            def _():
+                rows_arrived(slot + j).wait_recv()
+
+            return inner
+
+        lax.fori_loop(0, per, settle, 0)
+        rt_ref[...] = (v_ref[pl.ds(base, LANES), :] - got_ref[pl.ds(base, LANES), :]).T
+
+        def step(f, inner):
+            return score_step(f, inner, rt_ref, codes_ref, base, book_ref, w_ref)
+
+        finish(lax.fori_loop(0, steps, step, score_start(sub_width)), first, base)
+        return carry
+
+    lax.fori_loop(0, row_count * spans - 1, group_step, 0)
+
+    _, first, base = group_at(row_count * spans - 1)
+
+    def last_step(f, carry):
+        for j in range(per):
+            last_arrived(j, f).wait_recv()
+        part = pl.ds(pl.multiple_of(f * LANES, LANES), LANES)
+        rt_ref[part, :] = (v_ref[pl.ds(base, LANES), part] - got_ref[pl.ds(base, LANES), part]).T
+        return score_step(f, carry, rt_ref, codes_ref, base, book_ref, w_ref)
+
+    finish(lax.fori_loop(0, steps, last_step, score_start(sub_width)), first, base)
 
     @pl.when(spreads)
     def _():
-        for step in range(1, col_count):
-            first_copy(step).wait_send()
+        book_copy_to(col, mirror, first_send.at[0]).wait_send()
+        for copy in spread(col, first_send) + spread(mirror, mirror_send):
+            copy.wait_send()
 
     for group in range(groups):
         @pl.when(group * row_count + row != col)
@@ -300,12 +363,21 @@
             for step in range(1, row_count):
                 second_copy(group, step).wait_send()
 
-    def drain(slot, carry):
+    def drain_ids(slot, carry):
         ids_copy(slot).wait_send()
+        return carry
+
+    def drain_rows(slot, carry):
         rows_copy(slot).wait_send()
         return carry
 
-    lax.fori_loop(1, count, drain, 0)
+    def drain_last(i, carry):
+        last_copy(lax.rem(i, per), lax.div(i, per)).wait_send()
+        return carry
+
+    lax.fori_loop(1, count, drain_ids, 0)
+    lax.fori_loop(1, last, drain_rows, 0)
+    lax.fori_loop(0, per * steps, drain_last, 0)
 
 
 def local(vectors, list_ids, pq_codes, fill_counts, centroids, codebook):
@@ -315,14 +387,15 @@
     slot_count, feature_width = vectors.shape
     sub_total = pq_codes.shape[1]
     sub_width, code_count = codebook.shape[1:]
+    per = LANES * count // slot_count
     vmem = pl.BlockSpec(memory_space=pltpu.VMEM)
     smem = pl.BlockSpec(memory_space=pltpu.SMEM)
     hbm = pl.BlockSpec(memory_space=pl.ANY)
-    coded, best = pl.pallas_call(
+    coded, best, live = pl.pallas_call(
         functools.partial(exchange_kernel, row_count, col_count),
-        out_shape=[jax.ShapeDtypeStruct((1, slot_count), F32)] * 2,
+        out_shape=[jax.ShapeDtypeStruct((1, slot_count), kind) for kind in (F32, F32, jnp.int32)],
         in_specs=[hbm] * 4 + [vmem, smem],
-        out_specs=[vmem] * 2,
+        out_specs=[vmem] * 3,
         scratch_shapes=[
             pltpu.VMEM((slot_count, feature_width), F32),
             pltpu.VMEM((slot_count, feature_width), F32),
@@ -336,17 +409,21 @@
             pltpu.SemaphoreType.DMA((5,)),
             pltpu.SemaphoreType.DMA((count,)),
             pltpu.SemaphoreType.DMA((count,)),
-            pltpu.SemaphoreType.DMA((col_count,)),
+            pltpu.SemaphoreType.DMA((col_count // 2,)),
+            pltpu.SemaphoreType.DMA((col_count // 2,)),
             pltpu.SemaphoreType.DMA((col_count // row_count, row_count)),
             pltpu.SemaphoreType.DMA((col_count,)),
             pltpu.SemaphoreType.DMA((count,)),
             pltpu.SemaphoreType.DMA((count,)),
+            pltpu.SemaphoreType.DMA((feature_width // LANES, per)),
+            pltpu.SemaphoreType.DMA((feature_width // LANES, per)),
         ],
         compiler_params=pltpu.CompilerParams(
             collective_id=0, has_side_effects=True, vmem_limit_bytes=56 * 2**20),
         name="exchange_score",
     )(codebook, vectors, pq_codes.T, centroids, list_ids.reshape(slot_count // LANES, LANES), fill_counts)
-    return coded.reshape(slot_count), best.reshape(slot_count)
+    alive = live.reshape(slot_count) > 0
+    return jnp.where(alive, coded.reshape(slot_count), 0.0), jnp.where(alive, best.reshape(slot_count), 0.0)
 
 
 def solution(mesh):

time: 91.9 us -> 94.7 us (1.030)
  the two profiles are of different devices: /device:TPU:19 before, /device:TPU:17 now
where the time goes in v2:
time: 94.7 us; the launch traced here: 94.4 us
  Pallas kernels  92.5 us (98%)
  other arithmetic  1.29 us (1%)
    pallas_call x1, Pallas kernels, local(): pl.pallas_call(functools.partial(exchange_kernel, row_count, col_count),...  92.5 us

profile of v2, /device:TPU:17, one launch (start us, length us, event | category | flops | bytes accessed | tf_op | source)
XLA Modules:
  0.0 94.4 jit_solution(15953597851825743168)
XLA Ops:
  0.6 92.5 %exchange_score.1 = (f32[1,1024]{1,0:T(1,128)}, f32[1,1024]{1,0:T(1,128)}, s32[1,1024]{1,0:T(1,128)}) custom-call(f32[12,8,256]{2,1,0:T(8,128)} %cb_hbm.1, f32[1024,768]{1,0:T(8,128)} %v_hbm.1, s32[96,1024]{1,0:T(8,128)} %bitcast.4, f32[512,768]{1,0:T(8,128)} %cent_hbm.1, s32[8,128]{1,0:T(8,128)} %bitcast.5, s32[1,32]{1,0:T(1,128)} %fill_ref.1), custom_call_target="tpu_custom_call" | custom-call | tf_op jit(solution)/shard_map/exchange_score/pallas_call | solution.py:394
  93.2 1.3 %compare_select_fusion = (f32[1,1024]{1,0:T(1,128)}, f32[1,1024]{1,0:T(1,128)}) fusion(f32[1,1024]{1,0:T(1,128)} %get-tuple-element.7, s32[1,1024]{1,0:T(1,128)} %get-tuple-element.5, f32[1,1024]{1,0:T(1,128)} %get-tuple-element.6), kind=kLoop, calls=%fused_computation | loop fusion | flops 3072 | bytes 20480 | tf_op jit(solution)/shard_map/jit(_where)/select_n | solution.py:426

commit v3 on v2

--- a/solution.py
+++ b/solution.py
@@ -12,6 +12,7 @@
 DEPTH = 64
 LANES = 128
 PAIRS = 8
+SLICES = 2
 
 
 def xor(i, s, count):
@@ -118,6 +119,8 @@
     mirror = xor(col, top, col_count)
     steps = v_ref.shape[1] // LANES
     last = count - per
+    slice_width = v_ref.shape[1] // SLICES
+    slice_steps = steps // SLICES
 
     def place(slot):
         return xor(row, lax.div(slot, col_count), row_count), xor(col, lax.rem(slot, col_count), col_count)
@@ -227,7 +230,7 @@
 
     def last_copy(j, f):
         r, c = place(last + j)
-        part = pl.ds(pl.multiple_of(f * LANES, LANES), LANES)
+        part = pl.ds(pl.multiple_of(f * slice_width, LANES), slice_width)
         return pltpu.make_async_remote_copy(
             src_ref=block(wanted_ref, r * col_count + c).at[:, part], dst_ref=block(got_ref, me).at[:, part],
             send_sem=last_send.at[f, j], recv_sem=last_recv.at[f, j],
@@ -235,7 +238,7 @@
 
     def last_arrived(j, f):
         r, c = place(last + j)
-        part = pl.ds(pl.multiple_of(f * LANES, LANES), LANES)
+        part = pl.ds(pl.multiple_of(f * slice_width, LANES), slice_width)
         return pltpu.make_async_remote_copy(
             src_ref=block(wanted_ref, me).at[:, part], dst_ref=block(got_ref, r * col_count + c).at[:, part],
             send_sem=last_send.at[f, j], recv_sem=last_recv.at[f, j],
@@ -259,10 +262,10 @@
 
     cent_copy.wait()
     half = (row_count // 2) * col_count
-    serve(1, half)
+    serve(top, col_count)
     own_ids.wait()
     gather(me, got_ref)
-    rows_copy(half - 1).start()
+    rows_copy(col_count - 1).start()
 
     @pl.when(spreads)
     def _():
@@ -270,6 +273,11 @@
         for copy in spread(mirror, mirror_send):
             copy.start()
 
+    serve(1, top)
+    serve(col_count, half)
+    rows_copy(top - 1).start()
+    rows_copy(half - 1).start()
+
     for group in range(groups):
         j = group * row_count + row
 
@@ -290,7 +298,7 @@
         last_copy(lax.rem(i, per), lax.div(i, per)).start()
         return carry
 
-    lax.fori_loop(0, per * steps, send_last, 0)
+    lax.fori_loop(0, per * SLICES, send_last, 0)
 
     for group in range(groups):
         for step in range(1, row_count):
@@ -342,14 +350,18 @@
 
     _, first, base = group_at(row_count * spans - 1)
 
-    def last_step(f, carry):
+    carry = score_start(sub_width)
+    for f in range(SLICES):
         for j in range(per):
             last_arrived(j, f).wait_recv()
-        part = pl.ds(pl.multiple_of(f * LANES, LANES), LANES)
+        part = pl.ds(f * slice_width, slice_width)
         rt_ref[part, :] = (v_ref[pl.ds(base, LANES), part] - got_ref[pl.ds(base, LANES), part]).T
-        return score_step(f, carry, rt_ref, codes_ref, base, book_ref, w_ref)
-
-    finish(lax.fori_loop(0, steps, last_step, score_start(sub_width)), first, base)
+
+        def last_step(g, inner):
+            return score_step(g, inner, rt_ref, codes_ref, base, book_ref, w_ref)
+
+        carry = lax.fori_loop(f * slice_steps, (f + 1) * slice_steps, last_step, carry)
+    finish(carry, first, base)
 
     @pl.when(spreads)
     def _():
@@ -377,7 +389,7 @@
 
     lax.fori_loop(1, count, drain_ids, 0)
     lax.fori_loop(1, last, drain_rows, 0)
-    lax.fori_loop(0, per * steps, drain_last, 0)
+    lax.fori_loop(0, per * SLICES, drain_last, 0)
 
 
 def local(vectors, list_ids, pq_codes, fill_counts, centroids, codebook):
@@ -415,8 +427,8 @@
             pltpu.SemaphoreType.DMA((col_count,)),
             pltpu.SemaphoreType.DMA((count,)),
             pltpu.SemaphoreType.DMA((count,)),
-            pltpu.SemaphoreType.DMA((feature_width // LANES, per)),
-            pltpu.SemaphoreType.DMA((feature_width // LANES, per)),
+            pltpu.SemaphoreType.DMA((SLICES, per)),
+            pltpu.SemaphoreType.DMA((SLICES, per)),
         ],
         compiler_params=pltpu.CompilerParams(
             collective_id=0, has_side_effects=True, vmem_limit_bytes=56 * 2**20),

time: 94.7 us -> 87.4 us (0.923)
  the two profiles are of different devices: /device:TPU:17 before, /device:TPU:1 now
where the time goes in v3:
time: 87.4 us; the launch traced here: 86.8 us
  Pallas kernels  84.9 us (97%)
  other arithmetic  1.29 us (1%)
    pallas_call x1, Pallas kernels, local(): pl.pallas_call(functools.partial(exchange_kernel, row_count, col_count),...  84.9 us

profile of v3, /device:TPU:1, one launch (start us, length us, event | category | flops | bytes accessed | tf_op | source)
XLA Modules:
  0.0 86.8 jit_solution(17362372792167784310)
XLA Ops:
  0.6 84.9 %exchange_score.1 = (f32[1,1024]{1,0:T(1,128)}, f32[1,1024]{1,0:T(1,128)}, s32[1,1024]{1,0:T(1,128)}) custom-call(f32[12,8,256]{2,1,0:T(8,128)} %cb_hbm.1, f32[1024,768]{1,0:T(8,128)} %v_hbm.1, s32[96,1024]{1,0:T(8,128)} %bitcast.4, f32[512,768]{1,0:T(8,128)} %cent_hbm.1, s32[8,128]{1,0:T(8,128)} %bitcast.5, s32[1,32]{1,0:T(1,128)} %fill_ref.1), custom_call_target="tpu_custom_call" | custom-call | tf_op jit(solution)/shard_map/exchange_score/pallas_call | solution.py:406
  85.5 1.3 %compare_select_fusion = (f32[1,1024]{1,0:T(1,128)}, f32[1,1024]{1,0:T(1,128)}) fusion(f32[1,1024]{1,0:T(1,128)} %get-tuple-element.7, s32[1,1024]{1,0:T(1,128)} %get-tuple-element.5, f32[1,1024]{1,0:T(1,128)} %get-tuple-element.6), kind=kLoop, calls=%fused_computation | loop fusion | flops 3072 | bytes 20480 | tf_op jit(solution)/shard_map/jit(_where)/select_n | solution.py:438

commit v4 on v2

--- a/solution.py
+++ b/solution.py
@@ -100,8 +100,8 @@
 
 def exchange_kernel(row_count, col_count, cb_hbm, v_hbm, codes_hbm, cent_hbm, ids_ref, fill_ref,
                     coded_ref, best_ref, live_ref,
-                    wanted_ref, got_ref, v_ref, cent_ref, codes_ref, book_ref, w_ref, rt_ref, ids_sm,
-                    local_sem, ids_send, ids_recv, first_send, mirror_send, second_send, book_recv,
+                    wanted_ref, got_ref, v_ref, cent_ref, codes_ref, book_ref, w_ref, rt_ref, ids_own, ids_sm,
+                    local_sem, ready, ids_send, ids_recv, first_send, mirror_send, second_send, book_recv,
                     rows_send, rows_recv, last_send, last_recv):
     row = lax.axis_index("row")
     col = lax.axis_index("col")
@@ -111,13 +111,26 @@
     slot_count = v_ref.shape[0]
     capacity = slot_count // count
     lists = cent_ref.shape[0]
-    groups = col_count // row_count
     per = LANES // capacity
     spans = col_count // per
-    top = col_count // 2
-    mirror = xor(col, top, col_count)
     steps = v_ref.shape[1] // LANES
     last = count - per
+    cuts = (0, steps - steps // 3, steps)
+
+    top = col_count // 2
+    quarter = col_count // 4
+    zone = lax.div(col, quarter)
+    inner = zone * (3 - zone) > 0
+    outer = zone * (3 - zone) == 0
+    mirror = xor(col, top + quarter, col_count)
+    kin = row_count * top
+
+    def same_slot(i):
+        t = lax.rem(i, top)
+        return lax.div(i, top) * col_count + t + lax.div(t, quarter) * top
+
+    def cross_slot(i):
+        return lax.div(i, top) * col_count + quarter + lax.rem(i, top)
 
     def place(slot):
         return xor(row, lax.div(slot, col_count), row_count), xor(col, lax.rem(slot, col_count), col_count)
@@ -139,77 +152,111 @@
 
     barrier = pltpu.get_barrier_semaphore()
 
-    def greet(slot, carry):
+    for p in range(per):
+        ids = ids_ref[...]
+        ids_own[p] = ids if p == 0 else pltpu.roll(ids, LANES - p * capacity, 1)
+
+    def signal(sem, slot):
         r, c = place(slot)
-        pl.semaphore_signal(barrier, inc=1, device_id=(r, c), device_id_type=pl.DeviceIdType.MESH)
-        return carry
-
-    lax.fori_loop(1, count, greet, 0)
-    pl.semaphore_wait(barrier, count - 1)
+        pl.semaphore_signal(sem, inc=1, device_id=(r, c), device_id_type=pl.DeviceIdType.MESH)
+
+    def greet_same(i, carry):
+        signal(barrier, same_slot(i))
+        return carry
+
+    def greet_cross(i, carry):
+        signal(barrier, cross_slot(i))
+        return carry
+
+    def tell_cross(i, carry):
+        signal(ready, cross_slot(i))
+        return carry
+
+    lax.fori_loop(1, kin, greet_same, 0)
+
+    @pl.when(inner)
+    def _():
+        lax.fori_loop(0, kin, greet_cross, 0)
+        pl.semaphore_wait(barrier, kin - 1)
+
+    @pl.when(outer)
+    def _():
+        pl.semaphore_wait(barrier, count - 1)
+        lax.fori_loop(0, kin, tell_cross, 0)
+
+    def ids_of(owner):
+        return ids_own.at[lax.rem(owner, per), pl.ds(lax.div(owner, per), 1)]
 
     def ids_copy(slot):
         r, c = place(slot)
-        line = lax.div((r * col_count + c) * capacity, LANES)
-        return pltpu.make_async_remote_copy(
-            src_ref=ids_ref.at[pl.ds(line, 1)], dst_ref=ids_sm.at[pl.ds(me, 1)],
+        return pltpu.make_async_remote_copy(
+            src_ref=ids_of(r * col_count + c), dst_ref=ids_sm.at[pl.ds(me, 1)],
             send_sem=ids_send.at[slot], recv_sem=ids_recv.at[slot],
             device_id=(r, c), device_id_type=pl.DeviceIdType.MESH)
 
     def ids_arrived(slot):
         r, c = place(slot)
         return pltpu.make_async_remote_copy(
-            src_ref=ids_ref.at[pl.ds(0, 1)], dst_ref=ids_sm.at[pl.ds(r * col_count + c, 1)],
+            src_ref=ids_of(me), dst_ref=ids_sm.at[pl.ds(r * col_count + c, 1)],
             send_sem=ids_send.at[slot], recv_sem=ids_recv.at[slot],
             device_id=(r, c), device_id_type=pl.DeviceIdType.MESH)
 
-    def send_ids(i, carry):
-        ids_copy(count - 1 - i).start()
-        return carry
-
-    lax.fori_loop(0, count - 1, send_ids, 0)
+    def ids_same(i, carry):
+        ids_copy(same_slot(kin - 1 - i)).start()
+        return carry
+
+    def ids_cross(i, carry):
+        ids_copy(cross_slot(i)).start()
+        return carry
+
+    lax.fori_loop(0, kin - 1, ids_same, 0)
+
+    @pl.when(outer)
+    def _():
+        lax.fori_loop(0, kin, ids_cross, 0)
+
     own_ids = pltpu.make_async_copy(
-        ids_ref.at[pl.ds(lax.div(me * capacity, LANES), 1)], ids_sm.at[pl.ds(me, 1)], local_sem.at[4])
+        ids_of(me), ids_sm.at[pl.ds(me, 1)], local_sem.at[4])
     own_ids.start()
+
+    side = lax.rem(row, 2)
+    peer = row + 1 - 2 * side
 
     def book_copy_to(source, target, sem):
         return pltpu.make_async_remote_copy(
             src_ref=piece(source), dst_ref=piece(source), send_sem=sem, recv_sem=book_recv.at[source],
             device_id=(row, target), device_id_type=pl.DeviceIdType.MESH)
 
-    def second_copy(group, step):
-        j = group * row_count + row
-        return pltpu.make_async_remote_copy(
-            src_ref=piece(j), dst_ref=piece(j), send_sem=second_send.at[group, step], recv_sem=book_recv.at[j],
-            device_id=(lax.rem(row + step, row_count), col), device_id_type=pl.DeviceIdType.MESH)
+    def peer_copy(k):
+        j = 2 * k + side
+        return pltpu.make_async_remote_copy(
+            src_ref=piece(j), dst_ref=piece(j), send_sem=second_send.at[k], recv_sem=book_recv.at[j],
+            device_id=(peer, col), device_id_type=pl.DeviceIdType.MESH)
 
     def arrived(j):
         return book_copy_to(j, mirror, first_send.at[0])
 
-    def spread(source, sems):
-        return [book_copy_to(source, xor(col, b, col_count), sems.at[b]) for b in range(1, top)]
-
-    spreads = lax.rem(col, row_count) == row
+    def spread(source, sems, begin, end):
+        return [book_copy_to(source, xor(col, b, col_count), sems.at[b]) for b in range(begin, end)]
+
+    spreads = lax.rem(col, 2) == side
     book_copy.wait()
 
     @pl.when(spreads)
     def _():
-        book_copy_to(col, mirror, first_send.at[0]).start()
-        for copy in spread(col, first_send):
+        for copy in [book_copy_to(col, mirror, first_send.at[0])] + spread(col, first_send, 1, quarter):
             copy.start()
 
-    offset = lax.rem(me * capacity, LANES)
+        @pl.when(outer)
+        def _():
+            for copy in spread(col, first_send, quarter, top):
+                copy.start()
 
     def gather(owner, out_ref):
-        start = pl.multiple_of(owner * capacity, capacity)
-
-        def some(q, carry):
-            for k in range(8):
-                j = q * 8 + k
-                at = lax.rem(ids_sm[owner, offset + j], lists)
-                out_ref[pl.ds(start + j, 1), :] = cent_ref[pl.ds(at, 1), :]
-            return carry
-
-        lax.fori_loop(0, capacity // 8, some, 0)
+        out = block(out_ref, owner)
+        for j in range(capacity):
+            at = jnp.bitwise_and(ids_sm[owner, j], lists - 1)
+            out[pl.ds(j, 1), :] = cent_ref[pl.ds(at, 1), :]
 
     def rows_copy(slot):
         r, c = place(slot)
@@ -225,23 +272,26 @@
             send_sem=rows_send.at[slot], recv_sem=rows_recv.at[slot],
             device_id=(r, c), device_id_type=pl.DeviceIdType.MESH)
 
+    def last_part(f):
+        return pl.ds(cuts[f] * LANES, (cuts[f + 1] - cuts[f]) * LANES)
+
     def last_copy(j, f):
         r, c = place(last + j)
-        part = pl.ds(pl.multiple_of(f * LANES, LANES), LANES)
-        return pltpu.make_async_remote_copy(
-            src_ref=block(wanted_ref, r * col_count + c).at[:, part], dst_ref=block(got_ref, me).at[:, part],
+        return pltpu.make_async_remote_copy(
+            src_ref=block(wanted_ref, r * col_count + c).at[:, last_part(f)],
+            dst_ref=block(got_ref, me).at[:, last_part(f)],
             send_sem=last_send.at[f, j], recv_sem=last_recv.at[f, j],
             device_id=(r, c), device_id_type=pl.DeviceIdType.MESH)
 
     def last_arrived(j, f):
         r, c = place(last + j)
-        part = pl.ds(pl.multiple_of(f * LANES, LANES), LANES)
-        return pltpu.make_async_remote_copy(
-            src_ref=block(wanted_ref, me).at[:, part], dst_ref=block(got_ref, r * col_count + c).at[:, part],
+        return pltpu.make_async_remote_copy(
+            src_ref=block(wanted_ref, me).at[:, last_part(f)],
+            dst_ref=block(got_ref, r * col_count + c).at[:, last_part(f)],
             send_sem=last_send.at[f, j], recv_sem=last_recv.at[f, j],
             device_id=(r, c), device_id_type=pl.DeviceIdType.MESH)
 
-    def serve(first, end):
+    def serve(first, end, before=None):
         def one(slot, carry):
             r, c = place(slot)
             ids_arrived(slot).wait_recv()
@@ -253,52 +303,92 @@
                 def _():
                     rows_copy(slot - 1).start()
 
+            if before is not None:
+                @pl.when(slot == first)
+                def _():
+                    rows_copy(before).start()
+
             return carry
 
         lax.fori_loop(first, end, one, 0)
+        return end - 1
+
+    def forward():
+        arrived(mirror).wait_recv()
+        for copy in spread(mirror, mirror_send, 1, top):
+            copy.start()
+
+    @pl.when(outer)
+    def _():
+        @pl.when(spreads)
+        def _():
+            forward()
 
     cent_copy.wait()
-    half = (row_count // 2) * col_count
-    serve(1, half)
+    pending = serve(top + quarter, col_count)
     own_ids.wait()
     gather(me, got_ref)
-    rows_copy(half - 1).start()
-
-    @pl.when(spreads)
-    def _():
-        arrived(mirror).wait_recv()
-        for copy in spread(mirror, mirror_send):
-            copy.start()
-
-    for group in range(groups):
-        j = group * row_count + row
-
-        @pl.when((j - col) * (j - mirror) != 0)
-        def _(j=j):
-            arrived(j).wait_recv()
-
-        @pl.when(j != col)
-        def _(group=group):
-            for step in range(1, row_count):
-                second_copy(group, step).start()
-
-    serve(half, count)
+    rows_copy(pending).start()
+
+    @pl.when(inner)
+    def _():
+        pl.semaphore_wait(ready, kin)
+        lax.fori_loop(0, kin, ids_cross, 0)
+
+        @pl.when(spreads)
+        def _():
+            for copy in spread(col, first_send, quarter, top):
+                copy.start()
+            forward()
+
+    pending = serve(1, quarter)
+    for a in range(1, row_count // 2):
+        pending = serve(a * col_count + top + quarter, (a + 1) * col_count, pending)
+        pending = serve(a * col_count, a * col_count + quarter, pending)
     v_copy.wait()
     codes_copy.wait()
-
-    def send_last(i, carry):
-        last_copy(lax.rem(i, per), lax.div(i, per)).start()
-        return carry
-
-    lax.fori_loop(0, per * steps, send_last, 0)
-
-    for group in range(groups):
-        for step in range(1, row_count):
-            j = group * row_count + lax.rem(row - step + row_count, row_count)
-
-            @pl.when(j != col)
-            def _(j=j):
-                arrived(j).wait_recv()
+    rows_copy(pending).start()
+
+    def pass_on(k, carry):
+        j = 2 * k + side
+
+        @pl.when((j - col) * (j - mirror) != 0)
+        def _():
+            arrived(j).wait_recv()
+
+        @pl.when(j != col)
+        def _():
+            peer_copy(k).start()
+
+        return carry
+
+    lax.fori_loop(0, top, pass_on, 0)
+
+    pending = None
+    for a in range(row_count // 2):
+        pending = serve(a * col_count + quarter, a * col_count + top + quarter, pending)
+    serve((row_count // 2) * col_count, count, pending)
+
+    def send_last(f):
+        def one(j, carry):
+            last_copy(j, f).start()
+            return carry
+
+        lax.fori_loop(0, per, one, 0)
+
+    send_last(0)
+    send_last(1)
+
+    def from_peer(k, carry):
+        j = 2 * k + 1 - side
+
+        @pl.when(j != col)
+        def _():
+            arrived(j).wait_recv()
+
+        return carry
+
+    lax.fori_loop(0, top, from_peer, 0)
     build_table(book_ref, w_ref)
 
     lane = lax.broadcasted_iota(jnp.int32, (1, LANES), 1)
@@ -342,26 +432,33 @@
 
     _, first, base = group_at(row_count * spans - 1)
 
-    def last_step(f, carry):
+    carry = score_start(sub_width)
+    for f in range(2):
         for j in range(per):
             last_arrived(j, f).wait_recv()
-        part = pl.ds(pl.multiple_of(f * LANES, LANES), LANES)
+        part = last_part(f)
         rt_ref[part, :] = (v_ref[pl.ds(base, LANES), part] - got_ref[pl.ds(base, LANES), part]).T
-        return score_step(f, carry, rt_ref, codes_ref, base, book_ref, w_ref)
-
-    finish(lax.fori_loop(0, steps, last_step, score_start(sub_width)), first, base)
+
+        def last_step(g, inside):
+            return score_step(g, inside, rt_ref, codes_ref, base, book_ref, w_ref)
+
+        carry = lax.fori_loop(cuts[f], cuts[f + 1], last_step, carry)
+    finish(carry, first, base)
 
     @pl.when(spreads)
     def _():
         book_copy_to(col, mirror, first_send.at[0]).wait_send()
-        for copy in spread(col, first_send) + spread(mirror, mirror_send):
+        for copy in spread(col, first_send, 1, top) + spread(mirror, mirror_send, 1, top):
             copy.wait_send()
 
-    for group in range(groups):
-        @pl.when(group * row_count + row != col)
-        def _(group=group):
-            for step in range(1, row_count):
-                second_copy(group, step).wait_send()
+    def drain_peer(k, carry):
+        @pl.when(2 * k + side != col)
+        def _():
+            peer_copy(k).wait_send()
+
+        return carry
+
+    lax.fori_loop(0, top, drain_peer, 0)
 
     def drain_ids(slot, carry):
         ids_copy(slot).wait_send()
@@ -371,13 +468,14 @@
         rows_copy(slot).wait_send()
         return carry
 
-    def drain_last(i, carry):
-        last_copy(lax.rem(i, per), lax.div(i, per)).wait_send()
+    def drain_last(j, carry):
+        last_copy(j, 0).wait_send()
+        last_copy(j, 1).wait_send()
         return carry
 
     lax.fori_loop(1, count, drain_ids, 0)
     lax.fori_loop(1, last, drain_rows, 0)
-    lax.fori_loop(0, per * steps, drain_last, 0)
+    lax.fori_loop(0, per, drain_last, 0)
 
 
 def local(vectors, list_ids, pq_codes, fill_counts, centroids, codebook):
@@ -405,18 +503,20 @@
             pltpu.VMEM((sub_total, sub_width, code_count), F32),
             pltpu.VMEM((sub_total // 2, code_count, 2 * DEPTH), BF16),
             pltpu.VMEM((feature_width, LANES), F32),
+            pltpu.VMEM((per, slot_count // LANES, LANES), jnp.int32),
             pltpu.SMEM((count, LANES), jnp.int32),
             pltpu.SemaphoreType.DMA((5,)),
+            pltpu.SemaphoreType.REGULAR,
             pltpu.SemaphoreType.DMA((count,)),
             pltpu.SemaphoreType.DMA((count,)),
             pltpu.SemaphoreType.DMA((col_count // 2,)),
             pltpu.SemaphoreType.DMA((col_count // 2,)),
-            pltpu.SemaphoreType.DMA((col_count // row_count, row_count)),
+            pltpu.SemaphoreType.DMA((col_count // 2,)),
             pltpu.SemaphoreType.DMA((col_count,)),
             pltpu.SemaphoreType.DMA((count,)),
             pltpu.SemaphoreType.DMA((count,)),
-            pltpu.SemaphoreType.DMA((feature_width // LANES, per)),
-            pltpu.SemaphoreType.DMA((feature_width // LANES, per)),
+            pltpu.SemaphoreType.DMA((2, per)),
+            pltpu.SemaphoreType.DMA((2, per)),
         ],
         compiler_params=pltpu.CompilerParams(
             collective_id=0, has_side_effects=True, vmem_limit_bytes=56 * 2**20),

time: 94.7 us -> 84.6 us (0.89)
  the two profiles are of different devices: /device:TPU:17 before, /device:TPU:1 now
where the time goes in v4:
time: 84.6 us; the launch traced here: 84.4 us
  Pallas kernels  82.5 us (98%)
  other arithmetic  1.29 us (2%)
    pallas_call x1, Pallas kernels, local(): pl.pallas_call(functools.partial(exchange_kernel, row_count, col_count),...  82.5 us

profile of v4, /device:TPU:1, one launch (start us, length us, event | category | flops | bytes accessed | tf_op | source)
XLA Modules:
  0.0 84.4 jit_solution(12232270924303520452)
XLA Ops:
  0.6 82.5 %exchange_score.1 = (f32[1,1024]{1,0:T(1,128)}, f32[1,1024]{1,0:T(1,128)}, s32[1,1024]{1,0:T(1,128)}) custom-call(f32[12,8,256]{2,1,0:T(8,128)} %cb_hbm.1, f32[1024,768]{1,0:T(8,128)} %v_hbm.1, s32[96,1024]{1,0:T(8,128)} %bitcast.4, f32[512,768]{1,0:T(8,128)} %cent_hbm.1, s32[8,128]{1,0:T(8,128)} %bitcast.5, s32[1,32]{1,0:T(1,128)} %fill_ref.1), custom_call_target="tpu_custom_call" | custom-call | tf_op jit(solution)/shard_map/exchange_score/pallas_call | solution.py:492
  83.1 1.3 %compare_select_fusion = (f32[1,1024]{1,0:T(1,128)}, f32[1,1024]{1,0:T(1,128)}) fusion(f32[1,1024]{1,0:T(1,128)} %get-tuple-element.7, s32[1,1024]{1,0:T(1,128)} %get-tuple-element.5, f32[1,1024]{1,0:T(1,128)} %get-tuple-element.6), kind=kLoop, calls=%fused_computation | loop fusion | flops 3072 | bytes 20480 | tf_op jit(solution)/shard_map/jit(_where)/select_n | solution.py:526

commit v5 on v4

--- a/solution.py
+++ b/solution.py
@@ -98,9 +98,8 @@
     return coded, best[:, :LANES] + best[:, LANES:] + jnp.sum(norm, axis=0, keepdims=True)
 
 
-def exchange_kernel(row_count, col_count, cb_hbm, v_hbm, codes_hbm, cent_hbm, ids_ref, fill_ref,
-                    coded_ref, best_ref, live_ref,
-                    wanted_ref, got_ref, v_ref, cent_ref, codes_ref, book_ref, w_ref, rt_ref, ids_own, ids_sm,
+def exchange_kernel(row_count, col_count, cb_hbm, v_hbm, codes_hbm, cent_hbm, ids_hbm, fill_hbm, out_hbm,
+                    wanted_ref, got_ref, v_ref, cent_ref, codes_ref, book_ref, w_ref, rt_ref, out_ref, ids_ref, ids_own, fill_ref, ids_sm,
                     local_sem, ready, ids_send, ids_recv, first_send, mirror_send, second_send, book_recv,
                     rows_send, rows_recv, last_send, last_recv):
     row = lax.axis_index("row")
@@ -145,16 +144,18 @@
     book_copy = pltpu.make_async_copy(cb_hbm, piece(col), local_sem.at[1])
     v_copy = pltpu.make_async_copy(v_hbm, v_ref, local_sem.at[2])
     codes_copy = pltpu.make_async_copy(codes_hbm, codes_ref, local_sem.at[3])
+    ids_local = pltpu.make_async_copy(ids_hbm, ids_ref, local_sem.at[5])
+    fill_copy = pltpu.make_async_copy(fill_hbm, fill_ref, local_sem.at[6])
+    out_copy = pltpu.make_async_copy(out_ref, out_hbm, local_sem.at[7])
+    ids_local.start()
     book_copy.start()
     cent_copy.start()
     v_copy.start()
     codes_copy.start()
+    fill_copy.start()
 
     barrier = pltpu.get_barrier_semaphore()
 
-    for p in range(per):
-        ids = ids_ref[...]
-        ids_own[p] = ids if p == 0 else pltpu.roll(ids, LANES - p * capacity, 1)
 
     def signal(sem, slot):
         r, c = place(slot)
@@ -172,11 +173,22 @@
         signal(ready, cross_slot(i))
         return carry
 
+    def shift_ids():
+        ids_local.wait()
+        for p in range(per):
+            ids = ids_ref[...]
+            ids_own[p] = ids if p == 0 else pltpu.roll(ids, LANES - p * capacity, 1)
+
     lax.fori_loop(1, kin, greet_same, 0)
 
     @pl.when(inner)
     def _():
         lax.fori_loop(0, kin, greet_cross, 0)
+
+    shift_ids()
+
+    @pl.when(inner)
+    def _():
         pl.semaphore_wait(barrier, kin - 1)
 
     @pl.when(outer)
@@ -405,9 +417,9 @@
         bound = jnp.zeros((1, LANES), jnp.int32)
         for j in range(per):
             bound = jnp.where(lane >= j * capacity, fill_ref[0, first + j] + j * capacity, bound)
-        coded_ref[:, pl.ds(base, LANES)] = coded
-        best_ref[:, pl.ds(base, LANES)] = best
-        live_ref[:, pl.ds(base, LANES)] = jnp.where(lane < bound, 1, 0)
+        out_ref[0:1, pl.ds(base, LANES)] = coded
+        out_ref[1:2, pl.ds(base, LANES)] = best
+        out_ref[2:3, pl.ds(base, LANES)] = jnp.where(lane < bound, 1.0, 0.0)
 
     def group_step(g, carry):
         slot, first, base = group_at(g)
@@ -428,7 +440,29 @@
         finish(lax.fori_loop(0, steps, step, score_start(sub_width)), first, base)
         return carry
 
+    fill_copy.wait()
     lax.fori_loop(0, row_count * spans - 1, group_step, 0)
+
+    def sent(src, sem):
+        return pltpu.make_async_remote_copy(
+            src_ref=src, dst_ref=src, send_sem=sem, recv_sem=ids_recv.at[0],
+            device_id=(row, mirror), device_id_type=pl.DeviceIdType.MESH)
+
+    def drain_ids(slot, carry):
+        sent(ids_own.at[0, pl.ds(0, 1)], ids_send.at[slot]).wait_send()
+        return carry
+
+    def drain_rows(slot, carry):
+        sent(block(wanted_ref, 0), rows_send.at[slot]).wait_send()
+        return carry
+
+    def drain_last(j, carry):
+        for f in range(2):
+            sent(block(wanted_ref, 0).at[:, last_part(f)], last_send.at[f, j]).wait_send()
+        return carry
+
+    lax.fori_loop(1, count, drain_ids, 0)
+    lax.fori_loop(1, (row_count // 2) * col_count, drain_rows, 0)
 
     _, first, base = group_at(row_count * spans - 1)
 
@@ -460,22 +494,10 @@
 
     lax.fori_loop(0, top, drain_peer, 0)
 
-    def drain_ids(slot, carry):
-        ids_copy(slot).wait_send()
-        return carry
-
-    def drain_rows(slot, carry):
-        rows_copy(slot).wait_send()
-        return carry
-
-    def drain_last(j, carry):
-        last_copy(j, 0).wait_send()
-        last_copy(j, 1).wait_send()
-        return carry
-
-    lax.fori_loop(1, count, drain_ids, 0)
-    lax.fori_loop(1, last, drain_rows, 0)
+    lax.fori_loop((row_count // 2) * col_count, last, drain_rows, 0)
     lax.fori_loop(0, per, drain_last, 0)
+    out_copy.start()
+    out_copy.wait()
 
 
 def local(vectors, list_ids, pq_codes, fill_counts, centroids, codebook):
@@ -486,14 +508,12 @@
     sub_total = pq_codes.shape[1]
     sub_width, code_count = codebook.shape[1:]
     per = LANES * count // slot_count
-    vmem = pl.BlockSpec(memory_space=pltpu.VMEM)
-    smem = pl.BlockSpec(memory_space=pltpu.SMEM)
     hbm = pl.BlockSpec(memory_space=pl.ANY)
     coded, best, live = pl.pallas_call(
         functools.partial(exchange_kernel, row_count, col_count),
-        out_shape=[jax.ShapeDtypeStruct((1, slot_count), kind) for kind in (F32, F32, jnp.int32)],
-        in_specs=[hbm] * 4 + [vmem, smem],
-        out_specs=[vmem] * 3,
+        out_shape=jax.ShapeDtypeStruct((3, slot_count), F32),
+        in_specs=[hbm] * 6,
+        out_specs=hbm,
         scratch_shapes=[
             pltpu.VMEM((slot_count, feature_width), F32),
             pltpu.VMEM((slot_count, feature_width), F32),
@@ -503,9 +523,12 @@
             pltpu.VMEM((sub_total, sub_width, code_count), F32),
             pltpu.VMEM((sub_total // 2, code_count, 2 * DEPTH), BF16),
             pltpu.VMEM((feature_width, LANES), F32),
+            pltpu.VMEM((3, slot_count), F32),
+            pltpu.VMEM((slot_count // LANES, LANES), jnp.int32),
             pltpu.VMEM((per, slot_count // LANES, LANES), jnp.int32),
+            pltpu.SMEM(fill_counts.shape, jnp.int32),
             pltpu.SMEM((count, LANES), jnp.int32),
-            pltpu.SemaphoreType.DMA((5,)),
+            pltpu.SemaphoreType.DMA((8,)),
             pltpu.SemaphoreType.REGULAR,
             pltpu.SemaphoreType.DMA((count,)),
             pltpu.SemaphoreType.DMA((count,)),
@@ -522,8 +545,7 @@
             collective_id=0, has_side_effects=True, vmem_limit_bytes=56 * 2**20),
         name="exchange_score",
     )(codebook, vectors, pq_codes.T, centroids, list_ids.reshape(slot_count // LANES, LANES), fill_counts)
-    alive = live.reshape(slot_count) > 0
-    return jnp.where(alive, coded.reshape(slot_count), 0.0), jnp.where(alive, best.reshape(slot_count), 0.0)
+    return jnp.where(live > 0.0, coded, 0.0), jnp.where(live > 0.0, best, 0.0)
 
 
 def solution(mesh):

time: 84.6 us -> 83.4 us (0.986)
  Pallas kernels: 82.5 us -> 81.1 us
    pallas_call x1, Pallas kernels: 82.5 us -> 81.1 us  [local(): pl.pallas_call(functools.partial(exchange_kernel, row_count, col_count),...]
where the time goes in v5:
time: 83.4 us; the launch traced here: 83.2 us
  Pallas kernels  81.1 us (97%)
  other arithmetic  1.44 us (2%)
    pallas_call x1, Pallas kernels, local(): pl.pallas_call(functools.partial(exchange_kernel, row_count, col_count),...  81.1 us

profile of v5, /device:TPU:1, one launch (start us, length us, event | category | flops | bytes accessed | tf_op | source)
XLA Modules:
  0.0 83.2 jit_solution(17243595670348269123)
XLA Ops:
  0.6 81.1 %exchange_score.1 = f32[3,1024]{1,0:T(4,128)} custom-call(f32[12,8,256]{2,1,0:T(8,128)} %cb_hbm.1, f32[1024,768]{1,0:T(8,128)} %v_hbm.1, s32[96,1024]{1,0:T(8,128)} %bitcast.4, f32[512,768]{1,0:T(8,128)} %cent_hbm.1, s32[8,128]{1,0:T(8,128)} %bitcast.5, s32[1,32]{1,0:T(1,128)} %fill_hbm.1), custom_call_target="tpu_custom_call" | custom-call | tf_op jit(solution)/shard_map/exchange_score/pallas_call | solution.py:512
  81.8 1.4 %compare_select_fusion = (f32[1,1024]{1,0:T(1,128)}, f32[1,1024]{1,0:T(1,128)}) fusion(f32[3,1024]{1,0:T(4,128)} %exchange_score.1), kind=kLoop, calls=%fused_computation | loop fusion | flops 3072 | bytes 20480 | tf_op jit(solution)/shard_map/jit(_where)/select_n | solution.py:548

commit v6 on v5

--- a/solution.py
+++ b/solution.py
@@ -11,7 +11,7 @@
 BF16 = jnp.bfloat16
 DEPTH = 64
 LANES = 128
-PAIRS = 8
+PAIRS = 16
 
 
 def xor(i, s, count):
@@ -112,7 +112,8 @@
     lists = cent_ref.shape[0]
     per = LANES // capacity
     spans = col_count // per
-    steps = v_ref.shape[1] // LANES
+    width = 2 * PAIRS * cb_hbm.shape[1]
+    steps = v_ref.shape[1] // width
     last = count - per
     cuts = (0, steps - steps // 3, steps)
 
@@ -285,7 +286,7 @@
             device_id=(r, c), device_id_type=pl.DeviceIdType.MESH)
 
     def last_part(f):
-        return pl.ds(cuts[f] * LANES, (cuts[f + 1] - cuts[f]) * LANES)
+        return pl.ds(cuts[f] * width, (cuts[f + 1] - cuts[f]) * width)
 
     def last_copy(j, f):
         r, c = place(last + j)

time: 83.4 us -> 83.2 us (level)
  no operation moved by 1% of the time
where the time goes in v6:
time: 83.2 us; the launch traced here: 83 us
  Pallas kernels  80.9 us (97%)
  other arithmetic  1.44 us (2%)
    pallas_call x1, Pallas kernels, local(): pl.pallas_call(functools.partial(exchange_kernel, row_count, col_count),...  80.9 us

profile of v6, /device:TPU:1, one launch (start us, length us, event | category | flops | bytes accessed | tf_op | source)
XLA Modules:
  0.0 83.0 jit_solution(1095336658455392379)
XLA Ops:
  0.6 80.9 %exchange_score.1 = f32[3,1024]{1,0:T(4,128)} custom-call(f32[12,8,256]{2,1,0:T(8,128)} %cb_hbm.1, f32[1024,768]{1,0:T(8,128)} %v_hbm.1, s32[96,1024]{1,0:T(8,128)} %bitcast.4, f32[512,768]{1,0:T(8,128)} %cent_hbm.1, s32[8,128]{1,0:T(8,128)} %bitcast.5, s32[1,32]{1,0:T(1,128)} %fill_hbm.1), custom_call_target="tpu_custom_call" | custom-call | tf_op jit(solution)/shard_map/exchange_score/pallas_call | solution.py:513
  81.6 1.4 %compare_select_fusion = (f32[1,1024]{1,0:T(1,128)}, f32[1,1024]{1,0:T(1,128)}) fusion(f32[3,1024]{1,0:T(4,128)} %exchange_score.1), kind=kLoop, calls=%fused_computation | loop fusion | flops 3072 | bytes 20480 | tf_op jit(solution)/shard_map/jit(_where)/select_n | solution.py:549

commit v7 on v6

--- a/solution.py
+++ b/solution.py
@@ -101,7 +101,7 @@
 def exchange_kernel(row_count, col_count, cb_hbm, v_hbm, codes_hbm, cent_hbm, ids_hbm, fill_hbm, out_hbm,
                     wanted_ref, got_ref, v_ref, cent_ref, codes_ref, book_ref, w_ref, rt_ref, out_ref, ids_ref, ids_own, fill_ref, ids_sm,
                     local_sem, ready, ids_send, ids_recv, first_send, mirror_send, second_send, book_recv,
-                    rows_send, rows_recv, last_send, last_recv):
+                    rows_send, rows_recv, last_send, last_recv, out_sem):
     row = lax.axis_index("row")
     col = lax.axis_index("col")
     me = row * col_count + col
@@ -147,13 +147,7 @@
     codes_copy = pltpu.make_async_copy(codes_hbm, codes_ref, local_sem.at[3])
     ids_local = pltpu.make_async_copy(ids_hbm, ids_ref, local_sem.at[5])
     fill_copy = pltpu.make_async_copy(fill_hbm, fill_ref, local_sem.at[6])
-    out_copy = pltpu.make_async_copy(out_ref, out_hbm, local_sem.at[7])
     ids_local.start()
-    book_copy.start()
-    cent_copy.start()
-    v_copy.start()
-    codes_copy.start()
-    fill_copy.start()
 
     barrier = pltpu.get_barrier_semaphore()
 
@@ -186,7 +180,12 @@
     def _():
         lax.fori_loop(0, kin, greet_cross, 0)
 
+    book_copy.start()
+    cent_copy.start()
+    fill_copy.start()
     shift_ids()
+    v_copy.start()
+    codes_copy.start()
 
     @pl.when(inner)
     def _():
@@ -422,6 +421,14 @@
         out_ref[1:2, pl.ds(base, LANES)] = best
         out_ref[2:3, pl.ds(base, LANES)] = jnp.where(lane < bound, 1.0, 0.0)
 
+    def out_copy(g):
+        part = pl.ds(group_at(g)[2], LANES)
+        return pltpu.make_async_copy(out_ref.at[:, part], out_hbm.at[:, part], out_sem.at[g])
+
+    def out_wait(g, carry):
+        out_copy(g).wait()
+        return carry
+
     def group_step(g, carry):
         slot, first, base = group_at(g)
 
@@ -439,6 +446,11 @@
             return score_step(f, inner, rt_ref, codes_ref, base, book_ref, w_ref)
 
         finish(lax.fori_loop(0, steps, step, score_start(sub_width)), first, base)
+
+        @pl.when(g > 0)
+        def _():
+            out_copy(g - 1).start()
+
         return carry
 
     fill_copy.wait()
@@ -465,7 +477,9 @@
     lax.fori_loop(1, count, drain_ids, 0)
     lax.fori_loop(1, (row_count // 2) * col_count, drain_rows, 0)
 
-    _, first, base = group_at(row_count * spans - 1)
+    final = row_count * spans - 1
+    out_copy(final - 1).start()
+    _, first, base = group_at(final)
 
     carry = score_start(sub_width)
     for f in range(2):
@@ -496,9 +510,9 @@
     lax.fori_loop(0, top, drain_peer, 0)
 
     lax.fori_loop((row_count // 2) * col_count, last, drain_rows, 0)
+    out_copy(final).start()
     lax.fori_loop(0, per, drain_last, 0)
-    out_copy.start()
-    out_copy.wait()
+    lax.fori_loop(0, final + 1, out_wait, 0)
 
 
 def local(vectors, list_ids, pq_codes, fill_counts, centroids, codebook):
@@ -529,7 +543,7 @@
             pltpu.VMEM((per, slot_count // LANES, LANES), jnp.int32),
             pltpu.SMEM(fill_counts.shape, jnp.int32),
             pltpu.SMEM((count, LANES), jnp.int32),
-            pltpu.SemaphoreType.DMA((8,)),
+            pltpu.SemaphoreType.DMA((7,)),
             pltpu.SemaphoreType.REGULAR,
             pltpu.SemaphoreType.DMA((count,)),
             pltpu.SemaphoreType.DMA((count,)),
@@ -541,6 +555,7 @@
             pltpu.SemaphoreType.DMA((count,)),
             pltpu.SemaphoreType.DMA((2, per)),
             pltpu.SemaphoreType.DMA((2, per)),
+            pltpu.SemaphoreType.DMA((slot_count // LANES,)),
         ],
         compiler_params=pltpu.CompilerParams(
             collective_id=0, has_side_effects=True, vmem_limit_bytes=56 * 2**20),

time: 83.2 us -> 83.2 us (level)
  no operation moved by 1% of the time
where the time goes in v7:
time: 83.2 us; the launch traced here: 83 us
  Pallas kernels  80.9 us (97%)
  other arithmetic  1.44 us (2%)
    pallas_call x1, Pallas kernels, local(): pl.pallas_call(functools.partial(exchange_kernel, row_count, col_count),...  80.9 us

profile of v7, /device:TPU:1, one launch (start us, length us, event | category | flops | bytes accessed | tf_op | source)
XLA Modules:
  0.0 83.0 jit_solution(7006580457050217404)
XLA Ops:
  0.6 80.9 %exchange_score.1 = f32[3,1024]{1,0:T(4,128)} custom-call(f32[12,8,256]{2,1,0:T(8,128)} %cb_hbm.1, f32[1024,768]{1,0:T(8,128)} %v_hbm.1, s32[96,1024]{1,0:T(8,128)} %bitcast.4, f32[512,768]{1,0:T(8,128)} %cent_hbm.1, s32[8,128]{1,0:T(8,128)} %bitcast.5, s32[1,32]{1,0:T(1,128)} %fill_hbm.1), custom_call_target="tpu_custom_call" | custom-call | tf_op jit(solution)/shard_map/exchange_score/pallas_call | solution.py:527
  81.6 1.4 %compare_select_fusion = (f32[1,1024]{1,0:T(1,128)}, f32[1,1024]{1,0:T(1,128)}) fusion(f32[3,1024]{1,0:T(4,128)} %exchange_score.1), kind=kLoop, calls=%fused_computation | loop fusion | flops 3072 | bytes 20480 | tf_op jit(solution)/shard_map/jit(_where)/select_n | solution.py:564
